TPU v7x, 8 devices: a whole 2x2x1 slice. The times are simulated.
8 devices in a mesh: rep: 1 (over z), dp: 8 (over x, y, core).
Axes of the slice: x: 2, y: 2, z: 1, core: 2. Of those that a mesh axis runs over, the one named last changes fastest.
Arguments:
- x: bfloat16 [8, 2048, 1280], P(('rep', 'dp'))
- dy: bfloat16 [8, 2048, 1280], P(('rep', 'dp'))
- w_gate: bfloat16 [2, 1280, 4480], P(None, 'dp')
- w_up: bfloat16 [2, 1280, 4480], P(None, 'dp')
- w_down: bfloat16 [2, 4480, 1280], P(None, 'dp')
- m_w_gate: float32 [2, 1280, 4480], P(None, 'dp')
- m_w_up: float32 [2, 1280, 4480], P(None, 'dp')
- m_w_down: float32 [2, 4480, 1280], P(None, 'dp')
- v_w_gate: float32 [2, 1280, 4480], P(None, 'dp')
- v_w_up: float32 [2, 1280, 4480], P(None, 'dp')
- v_w_down: float32 [2, 4480, 1280], P(None, 'dp')
Outputs:
- output 1: bfloat16 [2, 1280, 4480], P('rep', 'dp')
- output 2: bfloat16 [2, 1280, 4480], P('rep', 'dp')
- output 3: bfloat16 [2, 4480, 1280], P('rep', 'dp')
- output 4: float32 [2, 1280, 4480], P('rep', 'dp')
- output 5: float32 [2, 1280, 4480], P('rep', 'dp')
- output 6: float32 [2, 4480, 1280], P('rep', 'dp')
- output 7: float32 [2, 1280, 4480], P('rep', 'dp')
- output 8: float32 [2, 1280, 4480], P('rep', 'dp')
- output 9: float32 [2, 4480, 1280], P('rep', 'dp')
All inputs are finite; a program needn't handle non-finite values.
Results may differ from a plain program's by a relative error of at most 0.022.
Values are sent between devices in bfloat16 or wider.
A program may use at most 2 GiB of HBM per device.

v0:
```python
import jax
import jax.numpy as jnp
from jax import lax
from jax.experimental import pallas as pl
from jax.experimental.pallas import tpu as pltpu
from jax.sharding import PartitionSpec as P

F32, BF16 = jnp.float32, jnp.bfloat16


def dot(a, w, dims=((1,), (0,))):
    return lax.dot_general(a, w, (dims, ((), ())), preferred_element_type=F32)


def scale_of(h):
    wide = h.astype(F32)
    return lax.rsqrt(jnp.mean(wide**2, -1, keepdims=True) + 1e-6)


def norm_back(by_a, h, scale):
    wide, by_a = h.astype(F32), by_a.astype(F32)
    by_scale = jnp.sum(by_a * wide, -1, keepdims=True)
    return by_a * scale - by_scale * scale**3 * wide / h.shape[-1]


def gates_back(by_hidden, gate, up):
    by = by_hidden.astype(F32)
    s = jax.nn.sigmoid(gate)
    return (by * up * (s * (1 + gate * (1 - s)))).astype(BF16), (by * (gate * s)).astype(BF16)


def adamw(w, m, v, g):
    m = 0.9 * m + 0.1 * g
    v = 0.95 * v + 0.05 * g * g
    step = m * lax.rsqrt(v + 1e-8) + 0.1 * w
    return (w - 0.02 * step).astype(BF16), m, v


def after(first, *rest):
    return lax.optimization_barrier((first, *rest))


MESH = pl.DeviceIdType.MESH
CORE, SIDE_Y, SIDE_X = 1, 2, 4
TILE = 640
ROWS = 256


def place():
    me = lax.axis_index("dp")
    bits = ((CORE, lax.rem(me, 2)), (SIDE_Y, lax.rem(me // 2, 2)), (SIDE_X, me // 4))

    def across(number, axes):
        for axis, bit in bits:
            if axes & axis:
                number = number + axis - 2 * axis * bit
        return number

    return me, across


def meet(me, across):
    barrier = pltpu.get_barrier_semaphore()
    for axis in (CORE, SIDE_Y, SIDE_X):
        pl.semaphore_signal(barrier, inc=1, device_id={"dp": across(me, axis)}, device_id_type=MESH)
    pl.semaphore_wait(barrier, 3)


class Gather:
    def __init__(self, me, across, shard, full, buffer, local, send, recv):
        self.me, self.across, self.shard, self.full, self.buffer = me, across, shard, full, buffer
        self.local, self.send, self.recv = local, send, recv
        self.rows = shard.shape[0]
        first = -(-self.rows // 32) * 16
        self.halves = ((0, first), (first, self.rows - first))
        self.sent = []

    def part(self, number, half):
        start, size = self.halves[half] if half is not None else (0, self.rows)
        return self.full.at[pl.ds(pl.multiple_of(number * self.rows + start, 16), size)]

    def remote(self, source, number, half, axis, slot):
        return pltpu.make_async_remote_copy(
            src_ref=source, dst_ref=self.part(number, half), send_sem=self.send.at[slot], recv_sem=self.recv.at[slot],
            device_id={"dp": self.across(self.me, axis)}, device_id_type=MESH,
        )

    def begin(self):
        pltpu.make_async_copy(self.shard, self.buffer, self.local.at[0]).start()
        for slot, half, axis in ((0, 0, SIDE_X), (2, 1, SIDE_Y), (1, 1, SIDE_X), (3, 0, SIDE_Y)):
            start, size = self.halves[half]
            copy = self.remote(self.shard.at[pl.ds(start, size)], self.me, half, axis, slot)
            copy.start()
            self.sent.append(copy)
        copy = self.remote(self.shard, self.me, None, CORE, 4)
        copy.start()
        self.sent.append(copy)

    def forward(self, number, half, axis, slot):
        copy = self.remote(self.part(number, half), number, half, axis, slot)
        copy.start()
        self.sent.append(copy)

    def got(self, number, half, slot):
        self.remote(self.part(number, half), number, half, CORE, slot).wait_recv()

    def relay(self):
        me, across = self.me, self.across
        pltpu.make_async_copy(self.shard, self.buffer, self.local.at[0]).wait()
        pltpu.make_async_copy(self.buffer, self.part(me, None), self.local.at[1]).start()
        self.got(across(me, SIDE_X), 0, 0)
        self.forward(across(me, SIDE_X), 0, SIDE_Y, 6)
        self.got(across(me, SIDE_Y), 1, 2)
        self.forward(across(me, SIDE_Y), 1, SIDE_X, 5)
        self.forward(across(me, SIDE_X), 0, CORE, 7)
        self.forward(across(me, SIDE_Y), 1, CORE, 8)

    def finish(self):
        me, across = self.me, self.across
        for axes, half, slot, on in ((SIDE_X, 1, 1, 9), (SIDE_Y, 0, 3, 10), (SIDE_X | SIDE_Y, 0, 6, 11), (SIDE_X | SIDE_Y, 1, 5, 12)):
            self.got(across(me, axes), half, slot)
            self.forward(across(me, axes), half, CORE, on)
        self.got(across(me, CORE), None, 4)
        for axes, half, slot in ((SIDE_X, 0, 7), (SIDE_Y, 1, 8), (SIDE_X, 1, 9), (SIDE_Y, 0, 10), (SIDE_X | SIDE_Y, 0, 11), (SIDE_X | SIDE_Y, 1, 12)):
            self.got(across(me, axes | CORE), half, slot)
        pltpu.make_async_copy(self.buffer, self.part(me, None), self.local.at[1]).wait()

    def close(self):
        for copy in self.sent:
            copy.wait_send()


def bring(source, target, sem):
    copy = pltpu.make_async_copy(source, target, sem)
    copy.start()
    copy.wait()


def forward_kernel(
    x, g, u, d, full_g0, full_u0, full_d0, full_g1, full_u1, full_d1, a0, gate0, up0, hidden0, h1, a1, gate1, up1, hidden1,
    states, down, small_a, small_b, wide_a, wide_b, local, send, recv, sem,
):
    me, across = place()
    order = (
        (g.at[0], full_g0, small_a), (u.at[0], full_u0, small_b), (d.at[0], full_d0, wide_a),
        (g.at[1], full_g1, small_a), (u.at[1], full_u1, small_b), (d.at[1], full_d1, wide_b),
    )
    gathers = [Gather(me, across, *refs, local.at[i], send.at[i], recv.at[i]) for i, refs in enumerate(order)]
    tokens, depth = states.shape
    wide = full_g0.shape[1]
    chunks = tokens // ROWS

    def rows(i):
        return pl.ds(pl.multiple_of(i * ROWS, ROWS), ROWS)

    def norm_of(value):
        value = value.astype(F32)
        return (value * lax.rsqrt(jnp.mean(value**2, -1, keepdims=True) + 1e-6)).astype(BF16)

    def gate_part(weight, gate, first, count):
        def body(w_tile, gate_tile):
            @pl.loop(0, chunks)
            def _(i):
                gate_tile[rows(i), :] = jnp.dot(states[rows(i), :], w_tile[...], preferred_element_type=F32)

        pltpu.emit_pipeline(
            body, grid=(count,),
            in_specs=[pl.BlockSpec((depth, TILE), lambda j: (0, j + first))],
            out_specs=[pl.BlockSpec((tokens, TILE), lambda j: (0, j + first))],
        )(weight, gate)

    def up_part(weight, gate, up, hidden, first, count):
        def body(w_tile, gate_tile, up_tile, hidden_tile):
            @pl.loop(0, chunks)
            def _(i):
                value = jnp.dot(states[rows(i), :], w_tile[...], preferred_element_type=F32)
                up_tile[rows(i), :] = value
                gate_value = gate_tile[rows(i), :]
                hidden_tile[rows(i), :] = (gate_value * jax.nn.sigmoid(gate_value) * value).astype(BF16)

        spec = pl.BlockSpec((tokens, TILE), lambda j: (0, j + first))
        pltpu.emit_pipeline(
            body, grid=(count,),
            in_specs=[pl.BlockSpec((depth, TILE), lambda j: (0, j + first)), spec],
            out_specs=[spec, spec],
        )(weight, gate, up, hidden)

    def down_part(first, count):
        def body(hidden_tile, x_tile, h_tile, a_tile):
            out = jnp.dot(hidden_tile[...], down[...], preferred_element_type=F32).astype(BF16)
            h = x_tile[...] + out
            h_tile[...] = h
            a_tile[...] = norm_of(h)

        spec = pl.BlockSpec((ROWS, depth), lambda i: (i + first, 0))
        pltpu.emit_pipeline(
            body, grid=(count,),
            in_specs=[pl.BlockSpec((ROWS, wide), lambda i: (i + first, 0)), spec],
            out_specs=[spec, spec],
        )(hidden0, x, h1, a1)

    meet(me, across)
    gathers[0].begin()
    bring(x.at[0] if x.ndim == 3 else x, states, sem)

    @pl.loop(0, chunks)
    def _(i):
        states[rows(i), :] = norm_of(states[rows(i), :])

    bring(states, a0, sem)

    def step(number, first_part, last_part):
        if first_part is not None:
            first_part()
        gathers[number].relay()
        if number + 1 < len(gathers):
            gathers[number + 1].begin()
        if last_part is not None:
            last_part()
        gathers[number].finish()

    tiles = wide // TILE
    most = (tiles + 1) // 2
    step(0, None, None)
    step(1, lambda: gate_part(full_g0, gate0, 0, most), lambda: gate_part(full_g0, gate0, most, tiles - most))
    step(2, lambda: up_part(full_u0, gate0, up0, hidden0, 0, most), lambda: up_part(full_u0, gate0, up0, hidden0, most, tiles - most))
    bring(full_d0, down, sem)
    step(3, lambda: down_part(0, chunks // 2), lambda: down_part(chunks // 2, chunks // 2))
    bring(a1, states, sem)
    step(4, lambda: gate_part(full_g1, gate1, 0, most), lambda: gate_part(full_g1, gate1, most, tiles - most))
    step(5, lambda: up_part(full_u1, gate1, up1, hidden1, 0, most), lambda: up_part(full_u1, gate1, up1, hidden1, most, tiles - most))
    for gather in gathers:
        gather.close()


def forward(x, w_gate, w_up, w_down):
    tokens, depth = x.shape
    wide = w_gate.shape[2]
    small, tall = (w_gate.shape[1], wide), (w_down.shape[1], depth)

    def array(shape, dtype=BF16):
        return jax.ShapeDtypeStruct(shape, dtype)

    into, out = array((depth, wide)), array((wide, depth))
    state, inner, inner32 = array((tokens, depth)), array((tokens, wide)), array((tokens, wide), F32)
    anywhere = pl.BlockSpec(memory_space=pl.ANY)
    shapes = [into, into, out, into, into, out, state, inner32, inner32, inner, state, state, inner32, inner32, inner]
    return pl.pallas_call(
        forward_kernel,
        name="forward",
        out_shape=shapes,
        in_specs=[anywhere] * 4,
        out_specs=[anywhere] * len(shapes),
        scratch_shapes=[
            pltpu.VMEM((tokens, depth), BF16), pltpu.VMEM((wide, depth), BF16),
            pltpu.VMEM(small, BF16), pltpu.VMEM(small, BF16), pltpu.VMEM(tall, BF16), pltpu.VMEM(tall, BF16),
            pltpu.SemaphoreType.DMA((6, 2)), pltpu.SemaphoreType.DMA((6, 13)), pltpu.SemaphoreType.DMA((6, 13)), pltpu.SemaphoreType.DMA,
        ],
        compiler_params=pltpu.CompilerParams(collective_id=0, has_side_effects=True, vmem_limit_bytes=66_000_000),
        cost_estimate=pl.CostEstimate(flops=10 * tokens * depth * wide, bytes_accessed=300_000_000, transcendentals=0),
    )(x, w_gate, w_up, w_down)


def solution(mesh):
    def scatter(g):
        return lax.psum_scatter(g, "dp", scatter_dimension=0, tiled=True)

    def step(x, dy, *arrays):
        weights, m, v = (arrays[i : i + 3] for i in (0, 3, 6))
        x, dy = x[0], dy[0]
        _, _, d0, g1, u1, d1, a0, gate0, up0, hidden0, h1, a1, gate1, up1, hidden1 = forward(x, *weights)
        s1 = scale_of(h1)

        rows = ((0,), (0,))
        by_d1 = dot(hidden1, dy, rows).astype(BF16)
        by_d1, dy_, gate1, up1 = after(by_d1, dy, gate1, up1)
        mine_d1 = scatter(by_d1)
        by_hidden1 = dot(dy_, d1, ((1,), (1,))).astype(BF16)
        by_gate1, by_up1 = after(*gates_back(by_hidden1, gate1, up1))
        by_g1 = dot(a1, by_gate1, rows).astype(BF16)
        by_g1, by_gate1, by_up1 = after(by_g1, by_gate1, by_up1)
        mine_g1 = scatter(by_g1)
        by_u1 = dot(a1, by_up1, rows).astype(BF16)
        by_u1, by_gate1, by_up1 = after(by_u1, by_gate1, by_up1)
        mine_u1 = scatter(by_u1)
        by_a1 = dot(by_gate1, g1, ((1,), (1,))).astype(BF16) + dot(by_up1, u1, ((1,), (1,))).astype(BF16)
        by_h1 = norm_back(by_a1, h1, s1).astype(BF16) + dy
        (by_h1,) = after(by_h1)
        by_d0 = dot(hidden0, by_h1, rows).astype(BF16)
        by_d0, by_h1, gate0, up0 = after(by_d0, by_h1, gate0, up0)
        mine_d0 = scatter(by_d0)
        by_hidden0 = dot(by_h1, d0, ((1,), (1,))).astype(BF16)
        by_gate0, by_up0 = after(*gates_back(by_hidden0, gate0, up0))
        by_g0 = dot(a0, by_gate0, rows).astype(BF16)
        by_g0, by_up0 = after(by_g0, by_up0)
        mine_g0 = scatter(by_g0)
        mine_u0 = scatter(dot(a0, by_up0, rows).astype(BF16))

        gradients = [jnp.stack(pair).astype(F32) for pair in ((mine_g0, mine_g1), (mine_u0, mine_u1), (mine_d0, mine_d1))]
        new = [adamw(w.astype(F32), m, v, g) for w, m, v, g in zip(weights, m, v, gradients, strict=True)]
        return tuple(one[which] for which in range(3) for one in new)

    states, cut = P(("rep", "dp"), None, None), P(None, "dp", None)
    return jax.shard_map(
        step,
        mesh=mesh,
        in_specs=(states, states) + (cut,) * 9,
        out_specs=(P("rep", "dp", None),) * 9,
        check_vma=False,
    )
```

profile of v0, /device:TPU:0, one launch (start us, length us, event | category | flops | bytes accessed | tf_op | source)
XLA Modules:
  0.0 1008.1 jit_solution(10469431231255748659)
XLA Ops:
  7.2 0.0 reduce-scatter.17.cloned.1.call-start
  7.2 325.6 %forward.1 = (bf16[1280,4480]{1,0:T(8,128)(2,1)}, bf16[1280,4480]{1,0:T(8,128)(2,1)}, bf16[4480,1280]{1,0:T(8,128)(2,1)}, bf16[1280,4480]{1,0:T(8,128)(2,1)}, bf...) custom-call(bf16[2048,1280]{1,0:T(8,128)(2,1)} %bitcast.37, ...), custom_call_target="tpu_custom_call" | custom-call | flops 117440512000 | bytes 300000000 | tf_op jit(solution)/shard_map/forward/pallas_call | solution.py:248
  332.8 30.6 %convolution_convert_fusion.7 = bf16[4480,1280]{1,0:T(8,128)(2,1)} fusion(bf16[2048,4480]{1,0:T(8,128)(2,1)} %get-tuple-element.45, bf16[1,2048,1280]{2,1,0:T(8,128)(2,1)} %param.12), kind=kOutput, calls=%fused_computation.19 | convolution fusion | flops 23493836800 | bytes 35061760 | tf_op jit(solution)/shard_map/dot_general | solution.py:12
  363.4 0.0 reduce-scatter.17.cloned.1.call-update
  363.4 0.0 reduce-scatter.15.cloned.1.call-start
  363.4 54.6 %fusion.2 = (bf16[2048,4480]{1,0:T(8,128)(2,1)}, bf16[2048,4480]{1,0:T(8,128)(2,1)}) fusion(f32[2048,4480]{1,0:T(8,128)} %get-tuple-element.51, f32[2048,4480]{1,0:T(8,128)} %get-tuple-element.50, bf16[2048,1280]{1,0:T(8,128)(2,1)} %bitcast.30, bf16[4480,1280]{1,0:T(8,128)(2,1)} %get-tuple-element.49), kind=kOutput, calls=%fused_computation.6 | convolution fusion | flops 23625728000 | bytes 126812160 | tf_op jit(solution)/shard_map/dot_general | solution.py:12
  418.0 31.7 %convolution_convert_fusion.4 = bf16[1280,4480]{1,0:T(8,128)(2,1)} fusion(bf16[2048,1280]{1,0:T(8,128)(2,1)} %get-tuple-element.44, bf16[2048,4480]{1,0:T(8,128)(2,1)} %get-tuple-element.56), kind=kOutput, calls=%fused_computation.16 | convolution fusion | flops 23493836800 | bytes 35061760 | tf_op jit(solution)/shard_map/dot_general | solution.py:12
  449.7 31.7 %convolution_convert_fusion.3 = bf16[1280,4480]{1,0:T(8,128)(2,1)} fusion(bf16[2048,1280]{1,0:T(8,128)(2,1)} %get-tuple-element.44, bf16[2048,4480]{1,0:T(8,128)(2,1)} %get-tuple-element.58), kind=kOutput, calls=%fused_computation.15 | convolution fusion | flops 23493836800 | bytes 35061760 | tf_op jit(solution)/shard_map/dot_general | solution.py:12
  481.4 31.8 %convolution_convert_fusion.8 = bf16[2048,1280]{1,0:T(8,128)(2,1)} fusion(bf16[2048,4480]{1,0:T(8,128)(2,1)} %get-tuple-element.58, bf16[1280,4480]{1,0:T(8,128)(2,1)} %get-tuple-element.59), kind=kOutput, calls=%fused_computation.32 | convolution fusion | flops 23490723840 | bytes 35061760 | tf_op jit(solution)/shard_map/dot_general | solution.py:12
  513.3 33.6 %fusion.8 = (f32[2048]{0:T(1024)S(1)}, f32[2048]{0:T(1024)S(1)}, bf16[2048,1280]{1,0:T(8,128)(2,1)}) fusion(bf16[2048,1280]{1,0:T(8,128)(2,1)} %get-tuple-element.60, bf16[2048,1280]{1,0:T(8,128)(2,1)} %convolution_convert_fusion.8, bf16[2048,4480]{1,0:T(8,128)(2,1)} %get-tuple-element.56, bf16[1280,4480]{1,0:T(8,128)(2,1)} %get-tuple-element.57), kind=kOutput, calls=%fused_computation.26 | convolution fusion | flops 23509069824 | bytes 45563904 | tf_op jit(solution)/shard_map/dot_general | solution.py:12
  546.9 7.4 fusion.27
  554.3 0.0 copy-start
  554.3 2.3 copy-done
  556.6 29.5 %convolution_convert_fusion.6 = bf16[4480,1280]{1,0:T(8,128)(2,1)} fusion(bf16[2048,4480]{1,0:T(8,128)(2,1)} %get-tuple-element.43, bf16[2048,1280]{1,0:T(8,128)(2,1)S(1)} %fusion.27), kind=kOutput, calls=%fused_computation.18 | convolution fusion | flops 23493836800 | bytes 35061760 | tf_op jit(solution)/shard_map/dot_general | solution.py:12
  586.1 0.0 reduce-scatter.15.cloned.1.call-update
  586.1 0.0 reduce-scatter.13.cloned.1.call-start
  586.2 0.7 reduce-scatter.13.cloned.1.call-update
  586.9 0.0 reduce-scatter.11.cloned.1.call-start
  586.9 57.9 %fusion.5 = (bf16[2048,4480]{1,0:T(8,128)(2,1)}, bf16[2048,4480]{1,0:T(8,128)(2,1)}) fusion(f32[2048,4480]{1,0:T(8,128)} %get-tuple-element.66, f32[2048,4480]{1,0:T(8,128)} %get-tuple-element.65, bf16[2048,1280]{1,0:T(8,128)(2,1)} %copy-done, bf16[4480,1280]{1,0:T(8,128)(2,1)} %get-tuple-element.64), kind=kOutput, calls=%fused_computation.9 | convolution fusion | flops 23625728000 | bytes 126812160 | tf_op jit(solution)/shard_map/dot_general | solution.py:12
  644.8 31.8 %convolution_convert_fusion.1 = bf16[1280,4480]{1,0:T(8,128)(2,1)} fusion(bf16[2048,1280]{1,0:T(8,128)(2,1)} %get-tuple-element.42, bf16[2048,4480]{1,0:T(8,128)(2,1)} %get-tuple-element.67), kind=kOutput, calls=%fused_computation.13 | convolution fusion | flops 23493836800 | bytes 35061760 | tf_op jit(solution)/shard_map/dot_general | solution.py:12
  676.6 33.7 %convolution_convert_fusion = bf16[1280,4480]{1,0:T(8,128)(2,1)} fusion(bf16[2048,1280]{1,0:T(8,128)(2,1)} %get-tuple-element.42, bf16[2048,4480]{1,0:T(8,128)(2,1)} %get-tuple-element.71), kind=kOutput, calls=%fused_computation.12 | convolution fusion | flops 23493836800 | bytes 35061760 | tf_op jit(solution)/shard_map/dot_general | solution.py:12
  710.3 0.0 reduce-scatter.11.cloned.1.call-update
  710.4 0.0 reduce-scatter.9.cloned.1.call-start
  710.4 0.5 reduce-scatter.9.cloned.1.call-update
  711.0 0.0 copy-start.1
  711.0 0.0 reduce-scatter.7.cloned.1.call-start
  711.0 0.5 reduce-scatter.7.cloned.1.call-update
  711.6 0.0 reduce-scatter.17.cloned.1.call-done
  711.6 0.0 reduce-scatter.15.cloned.1.call-done
  711.6 1.2 copy-done.1
  712.8 10.1 fusion.22
  722.9 22.8 %reduce-scatter.13.cloned.1.call-done = bf16[160,4480]{1,0:T(8,128)(2,1)} async-done(((bf16[1280,4480]{1,0:T(8,128)(2,1)}), bf16[160,4480]{1,0:T(8,128)(2,1)}) %reduce-scatter.13.cloned.1.call-update) | async-done | bytes 1433616 | tf_op jit(solution)/shard_map/reduce_scatter | solution.py:266
  745.7 81.8 %reduce-scatter.11.cloned.1.call-done = bf16[160,4480]{1,0:T(8,128)(2,1)} async-done(((bf16[1280,4480]{1,0:T(8,128)(2,1)}), bf16[160,4480]{1,0:T(8,128)(2,1)}) %reduce-scatter.11.cloned.1.call-update) | async-done | bytes 1433616 | tf_op jit(solution)/shard_map/reduce_scatter | solution.py:266
  827.5 0.0 copy-start.2
  827.5 13.1 %fusion.18 = (bf16[2,160,4480]{2,1,0:T(8,128)(2,1)}, f32[2,160,4480]{2,1,0:T(8,128)}, f32[2,160,4480]{2,1,0:T(8,128)}) fusion(bf16[2,160,4480]{2,1,0:T(8,128)(2,1)} %u.1, bf16[1,160,4480]{2,1,0:T(8,128)(2,1)} %bitcast.32, bf16[1,160,4480]{2,1,0:T(8,128)(2,1)} %bitcast.35, f32[2,160,4480]{2,1,0:T(8,128)} %param.20, f32[2,160,4480]{2,1,0:T(8,128)} %param.17), kind=kLoop, calls=%fused_computation.50 | loop fusion | flops 27238400 | bytes 31539200 | tf_op jit(solution)/shard_map/convert_element_type | solution.py:36
  840.7 68.7 %reduce-scatter.9.cloned.1.call-done = bf16[160,4480]{1,0:T(8,128)(2,1)} async-done(((bf16[1280,4480]{1,0:T(8,128)(2,1)}), bf16[160,4480]{1,0:T(8,128)(2,1)}) %reduce-scatter.9.cloned.1.call-update) | async-done | bytes 1433616 | tf_op jit(solution)/shard_map/reduce_scatter | solution.py:266
  909.4 81.8 %reduce-scatter.7.cloned.1.call-done = bf16[160,4480]{1,0:T(8,128)(2,1)} async-done(((bf16[1280,4480]{1,0:T(8,128)(2,1)}), bf16[160,4480]{1,0:T(8,128)(2,1)}) %reduce-scatter.7.cloned.1.call-update) | async-done | bytes 1433616 | tf_op jit(solution)/shard_map/reduce_scatter | solution.py:266
  991.2 0.0 copy-done.2
  991.2 9.8 fusion.14
  (1 shorter events, 0.0 us)
Async XLA Ops:
  7.2 704.4 %reduce-scatter.17.cloned.1.call-start = ((), (), s32[]{:S(2)}) async-start(), calls=%async_computation.11 | async-start | bytes 12902400 | tf_op jit(solution)/shard_map/reduce_scatter | solution.py:266
  363.4 348.2 %reduce-scatter.15.cloned.1.call-start = ((), (), s32[]{:S(2)}) async-start(), calls=%async_computation.10 | async-start | bytes 12902400 | tf_op jit(solution)/shard_map/reduce_scatter | solution.py:266
  554.3 2.4 copy-start
  586.1 159.6 %reduce-scatter.13.cloned.1.call-start = ((), (), s32[]{:S(2)}) async-start(), calls=%async_computation.9 | async-start | bytes 12902400 | tf_op jit(solution)/shard_map/reduce_scatter | solution.py:266
  586.9 240.7 %reduce-scatter.11.cloned.1.call-start = ((), (), s32[]{:S(2)}) async-start(), calls=%async_computation.8 | async-start | bytes 12902400 | tf_op jit(solution)/shard_map/reduce_scatter | solution.py:266
  710.4 199.0 %reduce-scatter.9.cloned.1.call-start = ((), (), s32[]{:S(2)}) async-start(), calls=%async_computation.7 | async-start | bytes 12902400 | tf_op jit(solution)/shard_map/reduce_scatter | solution.py:266
  711.0 1.8 copy-start.1
  711.0 280.2 %reduce-scatter.7.cloned.1.call-start = ((), (), s32[]{:S(2)}) async-start(), calls=%async_computation.6 | async-start | bytes 12902400 | tf_op jit(solution)/shard_map/reduce_scatter | solution.py:266
  827.5 163.7 %copy-start.2 = (bf16[2,160,4480]{2,1,0:T(8,128)(2,1)S(1)}, bf16[2,160,4480]{2,1,0:T(8,128)(2,1)}, u32[]{:S(2)}) copy-start(bf16[2,160,4480]{2,1,0:T(8,128)(2,1)} %g.1) | copy-start | bytes 8601604
Sparse Core Ops, SparseCore 0:
  363.5 78.4 reduce-scatter.16
  586.2 77.4 reduce-scatter.14
  667.1 78.5 reduce-scatter.12
  749.0 78.5 reduce-scatter.10
  830.8 78.5 reduce-scatter.8
  912.7 78.5 reduce-scatter.6
where the time goes:
time: 1020 us; the launch traced here: 1010 us
  matrix products  367 us (36%)
  Pallas kernels  326 us (32%)
  waiting for transfers between devices  257 us (25%)
  other arithmetic  40.4 us (4%)
  between operations  14.4 us (1%)
    dot_general x10, matrix products, dot(): return lax.dot_general(a, w, (dims, ((), ())), preferred_element_type=F32)  367 us
    pallas_call x1, Pallas kernels, forward(): pl.pallas_call(forward_kernel, name='forward', out_shape=shapes, in_specs...  326 us
    reduce_scatter x6, waiting for transfers between devices, scatter(): return lax.psum_scatter(g, 'dp', scatter_dimension=0, tiled=True)  255 us
    convert_element_type x3, other arithmetic, adamw(): return ((w - 0.02 * step).astype(BF16), m, v)  33 us
  transfers between devices with their start and end apart: 6, of which 4 were waited for; matrix products, arithmetic and copies ran while one was open for 36% of the time, Pallas kernels for 0%

commit v1 on v0

--- a/solution.py
+++ b/solution.py
@@ -44,6 +44,7 @@
 CORE, SIDE_Y, SIDE_X = 1, 2, 4
 TILE = 640
 ROWS = 256
+TALL = 1024
 
 
 def place():
@@ -153,15 +154,18 @@
     def rows(i):
         return pl.ds(pl.multiple_of(i * ROWS, ROWS), ROWS)
 
+    def tall(i):
+        return pl.ds(pl.multiple_of(i * TALL, TALL), TALL)
+
     def norm_of(value):
         value = value.astype(F32)
         return (value * lax.rsqrt(jnp.mean(value**2, -1, keepdims=True) + 1e-6)).astype(BF16)
 
     def gate_part(weight, gate, first, count):
         def body(w_tile, gate_tile):
-            @pl.loop(0, chunks)
+            @pl.loop(0, tokens // TALL)
             def _(i):
-                gate_tile[rows(i), :] = jnp.dot(states[rows(i), :], w_tile[...], preferred_element_type=F32)
+                gate_tile[tall(i), :] = jnp.dot(states[tall(i), :], w_tile[...], preferred_element_type=F32)
 
         pltpu.emit_pipeline(
             body, grid=(count,),
@@ -171,12 +175,12 @@
 
     def up_part(weight, gate, up, hidden, first, count):
         def body(w_tile, gate_tile, up_tile, hidden_tile):
-            @pl.loop(0, chunks)
+            @pl.loop(0, tokens // TALL)
             def _(i):
-                value = jnp.dot(states[rows(i), :], w_tile[...], preferred_element_type=F32)
-                up_tile[rows(i), :] = value
-                gate_value = gate_tile[rows(i), :]
-                hidden_tile[rows(i), :] = (gate_value * jax.nn.sigmoid(gate_value) * value).astype(BF16)
+                value = jnp.dot(states[tall(i), :], w_tile[...], preferred_element_type=F32)
+                up_tile[tall(i), :] = value
+                gate_value = gate_tile[tall(i), :]
+                hidden_tile[tall(i), :] = (gate_value * jax.nn.sigmoid(gate_value) * value).astype(BF16)
 
         spec = pl.BlockSpec((tokens, TILE), lambda j: (0, j + first))
         pltpu.emit_pipeline(
@@ -259,6 +263,181 @@
         compiler_params=pltpu.CompilerParams(collective_id=0, has_side_effects=True, vmem_limit_bytes=66_000_000),
         cost_estimate=pl.CostEstimate(flops=10 * tokens * depth * wide, bytes_accessed=300_000_000, transcendentals=0),
     )(x, w_gate, w_up, w_down)
+
+
+HELD, SLOTS = 6, 4
+
+
+def sums_kernel(a, by_gate, by_up, mine_g, mine_u, states, tiles, terms, out, core_out, core_in, far_out, far_in, near_out, near_in, local, core_s, core_r, far_s, far_r, near_s, near_r):
+    me, across = place()
+    _, depth = states.shape
+    block = depth // 8
+    half = block // 2
+    count = by_gate.shape[1] // TILE
+    sources, outs = (by_gate, by_up), (mine_g, mine_u)
+
+    def columns(j):
+        return pl.ds(pl.multiple_of(j * TILE, 128), TILE)
+
+    def load(p, j):
+        return pltpu.make_async_copy(sources[p].at[:, columns(j)], tiles.at[p], local.at[p])
+
+    def rows(number, start=0, size=block):
+        return pl.ds(pl.multiple_of(number * block + start, 16), size)
+
+    def core_copy(slot):
+        return pltpu.make_async_remote_copy(
+            src_ref=core_out.at[slot], dst_ref=core_in.at[slot], send_sem=core_s.at[slot], recv_sem=core_r.at[slot],
+            device_id={"dp": across(me, CORE)}, device_id_type=MESH,
+        )
+
+    def side_copy(source, target, sent, come, slot, side):
+        return pltpu.make_async_remote_copy(
+            src_ref=source.at[slot, side], dst_ref=target.at[slot, side], send_sem=sent.at[slot, side], recv_sem=come.at[slot, side],
+            device_id={"dp": across(me, (SIDE_X, SIDE_Y)[side])}, device_id_type=MESH,
+        )
+
+    def far_copy(slot, side):
+        return side_copy(far_out, far_in, far_s, far_r, slot, side)
+
+    def near_copy(slot, side):
+        return side_copy(near_out, near_in, near_s, near_r, slot, side)
+
+    blocks = (0, SIDE_X, SIDE_Y, SIDE_X | SIDE_Y)
+
+    def multiply(t, p, j):
+        load(p, j).wait()
+        held = lax.rem(t, HELD)
+
+        @pl.loop(0, depth // TILE)
+        def _(i):
+            part = pl.ds(pl.multiple_of(i * TILE, TILE), TILE)
+            terms[held, part, :] = lax.dot_general(
+                states[:, part], tiles[p], (((0,), (0,)), ((), ())), preferred_element_type=F32
+            )
+
+        @pl.when(j + 1 < count)
+        def _():
+            load(p, j + 1).start()
+
+    def to_core(t):
+        slot, held = lax.rem(t, SLOTS), lax.rem(t, HELD)
+
+        @pl.when(t >= SLOTS)
+        def _():
+            core_copy(slot).wait_send()
+
+        for i, axes in enumerate(blocks):
+            core_out[slot, i] = terms[held, rows(across(me, axes | CORE)), :].astype(BF16)
+        core_copy(slot).start()
+
+    def to_far(t):
+        slot, held = lax.rem(t, SLOTS), lax.rem(t, HELD)
+        core_copy(slot).wait_recv()
+
+        @pl.when(t >= SLOTS)
+        def _():
+            far_copy(slot, 0).wait_send()
+            far_copy(slot, 1).wait_send()
+
+        last = terms[held, rows(across(me, blocks[3])), :] + core_in[slot, 3].astype(F32)
+        for side in (0, 1):
+            far_out[slot, side] = last[side * half : (side + 1) * half].astype(BF16)
+            far_copy(slot, side).start()
+        for i, axes in enumerate(blocks[:3]):
+            terms[held, rows(across(me, axes)), :] += core_in[slot, i].astype(F32)
+
+    def to_near(t):
+        slot, held = lax.rem(t, SLOTS), lax.rem(t, HELD)
+        far_copy(slot, 0).wait_recv()
+        far_copy(slot, 1).wait_recv()
+
+        @pl.when(t >= SLOTS)
+        def _():
+            near_copy(slot, 0).wait_send()
+            near_copy(slot, 1).wait_send()
+
+        for side in (0, 1):
+            number = across(me, (SIDE_X, SIDE_Y)[side])
+            extra, plain = (half, 0) if side == 0 else (0, half)
+            near_out[slot, side, pl.ds(plain, half)] = terms[held, rows(number, plain, half), :].astype(BF16)
+            near_out[slot, side, pl.ds(extra, half)] = (
+                terms[held, rows(number, extra, half), :] + far_in[slot, 1 - side].astype(F32)
+            ).astype(BF16)
+        near_copy(slot, 0).start()
+        near_copy(slot, 1).start()
+
+    def to_out(t, p, j):
+        slot, held = lax.rem(t, SLOTS), lax.rem(t, HELD)
+        near_copy(slot, 0).wait_recv()
+        near_copy(slot, 1).wait_recv()
+        total = terms[held, rows(me), :] + near_in[slot, 0].astype(F32) + near_in[slot, 1].astype(F32)
+        out[p, :, columns(j)] = total.astype(BF16)
+
+    meet(me, across)
+    load(0, 0).start()
+    load(1, 0).start()
+    bring(a, states, local.at[2])
+
+    @pl.loop(0, count + 3)
+    def _(j):
+        for p in (0, 1):
+            t = 2 * j + p
+
+            @pl.when(j < count)
+            def _():
+                multiply(t, p, j)
+
+            def stage(lag, run):
+                q = (p - lag) % 2
+                behind = (lag - p + q) // 2
+
+                @pl.when((j >= behind) & (j - behind < count))
+                def _():
+                    run(t - lag, q, j - behind)
+
+            stage(5, to_out)
+            stage(3, lambda t, q, j: to_near(t))
+            stage(1, lambda t, q, j: to_far(t))
+
+            @pl.when(j < count)
+            def _():
+                to_core(t)
+
+    for slot in range(SLOTS):
+        core_copy(slot).wait_send()
+        for side in (0, 1):
+            far_copy(slot, side).wait_send()
+            near_copy(slot, side).wait_send()
+    for p in (0, 1):
+        bring(out.at[p], outs[p], local.at[2])
+
+
+def sums(a, by_gate, by_up):
+    tokens, depth = a.shape
+    wide = by_gate.shape[1]
+    block = depth // 8
+    anywhere = pl.BlockSpec(memory_space=pl.ANY)
+    return pl.pallas_call(
+        sums_kernel,
+        name="sums",
+        out_shape=[jax.ShapeDtypeStruct((block, wide), BF16)] * 2,
+        in_specs=[anywhere] * 3,
+        out_specs=[anywhere] * 2,
+        scratch_shapes=[
+            pltpu.VMEM((tokens, depth), BF16), pltpu.VMEM((2, tokens, TILE), BF16), pltpu.VMEM((HELD, depth, TILE), F32),
+            pltpu.VMEM((2, block, wide), BF16),
+            pltpu.VMEM((SLOTS, 4, block, TILE), BF16), pltpu.VMEM((SLOTS, 4, block, TILE), BF16),
+            pltpu.VMEM((SLOTS, 2, block // 2, TILE), BF16), pltpu.VMEM((SLOTS, 2, block // 2, TILE), BF16),
+            pltpu.VMEM((SLOTS, 2, block, TILE), BF16), pltpu.VMEM((SLOTS, 2, block, TILE), BF16),
+            pltpu.SemaphoreType.DMA((3,)),
+            pltpu.SemaphoreType.DMA((SLOTS,)), pltpu.SemaphoreType.DMA((SLOTS,)),
+            pltpu.SemaphoreType.DMA((SLOTS, 2)), pltpu.SemaphoreType.DMA((SLOTS, 2)),
+            pltpu.SemaphoreType.DMA((SLOTS, 2)), pltpu.SemaphoreType.DMA((SLOTS, 2)),
+        ],
+        compiler_params=pltpu.CompilerParams(collective_id=1, has_side_effects=True, vmem_limit_bytes=66_000_000),
+        cost_estimate=pl.CostEstimate(flops=4 * tokens * depth * wide, bytes_accessed=60_000_000, transcendentals=0),
+    )(a, by_gate, by_up)
 
 
 def solution(mesh):
@@ -291,10 +470,7 @@
         mine_d0 = scatter(by_d0)
         by_hidden0 = dot(by_h1, d0, ((1,), (1,))).astype(BF16)
         by_gate0, by_up0 = after(*gates_back(by_hidden0, gate0, up0))
-        by_g0 = dot(a0, by_gate0, rows).astype(BF16)
-        by_g0, by_up0 = after(by_g0, by_up0)
-        mine_g0 = scatter(by_g0)
-        mine_u0 = scatter(dot(a0, by_up0, rows).astype(BF16))
+        mine_g0, mine_u0 = sums(a0, by_gate0, by_up0)
 
         gradients = [jnp.stack(pair).astype(F32) for pair in ((mine_g0, mine_g1), (mine_u0, mine_u1), (mine_d0, mine_d1))]
         new = [adamw(w.astype(F32), m, v, g) for w, m, v, g in zip(weights, m, v, gradients, strict=True)]

time: 1020 us -> 884 us (0.87)
  waiting for transfers between devices: 257 us -> 46.7 us
  Pallas kernels: 326 us -> 466 us
  matrix products: 367 us -> 301 us
    reduce_scatter x6 -> x4, waiting for transfers between devices: 255 us -> 45.4 us  [scatter(): return lax.psum_scatter(g, 'dp', scatter_dimension=0, tiled=True)]
    pallas_call x0 -> x1, Pallas kernels: none -> 163 us  [sums(): pl.pallas_call(sums_kernel, name='sums', out_shape=[jax.ShapeDtypeStruct(...]
    dot_general x10 -> x8, matrix products: 367 us -> 301 us  [dot(): return lax.dot_general(a, w, (dims, ((), ())), preferred_element_type=F32)]
    pallas_call x1, Pallas kernels: 326 us -> 303 us  [forward(): pl.pallas_call(forward_kernel, name='forward', out_shape=shapes, in_specs...]
  transfers between devices with their start and end apart: 6 -> 4, of which waited for: 4 -> 1; matrix products, arithmetic and copies ran while one was open for 36% -> 35% of each run, Pallas kernels for 0% -> 19%
where the time goes in v1:
time: 884 us; the launch traced here: 875 us
  Pallas kernels  466 us (53%)
  matrix products  301 us (34%)
  waiting for transfers between devices  46.7 us (5%)
  other arithmetic  44.7 us (5%)
  between operations  14.3 us (2%)
    pallas_call x1, Pallas kernels, forward(): pl.pallas_call(forward_kernel, name='forward', out_shape=shapes, in_specs...  303 us
    dot_general x8, matrix products, dot(): return lax.dot_general(a, w, (dims, ((), ())), preferred_element_type=F32)  301 us
    pallas_call x1, Pallas kernels, sums(): pl.pallas_call(sums_kernel, name='sums', out_shape=[jax.ShapeDtypeStruct(...  163 us
    reduce_scatter x4, waiting for transfers between devices, scatter(): return lax.psum_scatter(g, 'dp', scatter_dimension=0, tiled=True)  45.4 us
    convert_element_type x3, other arithmetic, adamw(): return ((w - 0.02 * step).astype(BF16), m, v)  37.2 us
  transfers between devices with their start and end apart: 4, of which 1 were waited for; matrix products, arithmetic and copies ran while one was open for 35% of the time, Pallas kernels for 19%

profile of v1, /device:TPU:0, one launch (start us, length us, event | category | flops | bytes accessed | tf_op | source)
XLA Modules:
  0.0 875.4 jit_solution(8730483282420919453)
XLA Ops:
  7.2 0.0 reduce-scatter.11.cloned.1.call-start
  7.2 303.0 %forward.1 = (bf16[1280,4480]{1,0:T(8,128)(2,1)}, bf16[1280,4480]{1,0:T(8,128)(2,1)}, bf16[4480,1280]{1,0:T(8,128)(2,1)}, bf16[1280,4480]{1,0:T(8,128)(2,1)}, bf...) custom-call(bf16[2048,1280]{1,0:T(8,128)(2,1)} %bitcast.33, ...), custom_call_target="tpu_custom_call" | custom-call | flops 117440512000 | bytes 300000000 | tf_op jit(solution)/shard_map/forward/pallas_call | solution.py:252
  310.3 30.0 %convolution_convert_fusion.5 = bf16[4480,1280]{1,0:T(8,128)(2,1)} fusion(bf16[2048,4480]{1,0:T(8,128)(2,1)} %get-tuple-element.45, bf16[1,2048,1280]{2,1,0:T(8,128)(2,1)} %param.12), kind=kOutput, calls=%fused_computation.17 | convolution fusion | flops 23493836800 | bytes 35061760 | tf_op jit(solution)/shard_map/dot_general | solution.py:12
  340.3 0.0 reduce-scatter.11.cloned.1.call-update
  340.3 0.0 reduce-scatter.9.cloned.1.call-start
  340.4 54.8 %fusion.2 = (bf16[2048,4480]{1,0:T(8,128)(2,1)}, bf16[2048,4480]{1,0:T(8,128)(2,1)}) fusion(f32[2048,4480]{1,0:T(8,128)} %get-tuple-element.51, f32[2048,4480]{1,0:T(8,128)} %get-tuple-element.50, bf16[2048,1280]{1,0:T(8,128)(2,1)} %bitcast.26, bf16[4480,1280]{1,0:T(8,128)(2,1)} %get-tuple-element.49), kind=kOutput, calls=%fused_computation.6 | convolution fusion | flops 23625728000 | bytes 126812160 | tf_op jit(solution)/shard_map/dot_general | solution.py:12
  395.2 31.6 %convolution_convert_fusion.2 = bf16[1280,4480]{1,0:T(8,128)(2,1)} fusion(bf16[2048,1280]{1,0:T(8,128)(2,1)} %get-tuple-element.44, bf16[2048,4480]{1,0:T(8,128)(2,1)} %get-tuple-element.56), kind=kOutput, calls=%fused_computation.14 | convolution fusion | flops 23493836800 | bytes 35061760 | tf_op jit(solution)/shard_map/dot_general | solution.py:12
  426.7 31.9 %convolution_convert_fusion.1 = bf16[1280,4480]{1,0:T(8,128)(2,1)} fusion(bf16[2048,1280]{1,0:T(8,128)(2,1)} %get-tuple-element.44, bf16[2048,4480]{1,0:T(8,128)(2,1)} %get-tuple-element.58), kind=kOutput, calls=%fused_computation.13 | convolution fusion | flops 23493836800 | bytes 35061760 | tf_op jit(solution)/shard_map/dot_general | solution.py:12
  458.6 31.8 %convolution_convert_fusion.6 = bf16[2048,1280]{1,0:T(8,128)(2,1)} fusion(bf16[2048,4480]{1,0:T(8,128)(2,1)} %get-tuple-element.58, bf16[1280,4480]{1,0:T(8,128)(2,1)} %get-tuple-element.59), kind=kOutput, calls=%fused_computation.30 | convolution fusion | flops 23490723840 | bytes 35061760 | tf_op jit(solution)/shard_map/dot_general | solution.py:12
  490.4 33.5 %fusion.8 = (f32[2048]{0:T(1024)S(1)}, f32[2048]{0:T(1024)S(1)}, bf16[2048,1280]{1,0:T(8,128)(2,1)}) fusion(bf16[2048,1280]{1,0:T(8,128)(2,1)} %get-tuple-element.60, bf16[2048,1280]{1,0:T(8,128)(2,1)} %convolution_convert_fusion.6, bf16[2048,4480]{1,0:T(8,128)(2,1)} %get-tuple-element.56, bf16[1280,4480]{1,0:T(8,128)(2,1)} %get-tuple-element.57), kind=kOutput, calls=%fused_computation.24 | convolution fusion | flops 23509069824 | bytes 45563904 | tf_op jit(solution)/shard_map/dot_general | solution.py:12
  523.9 7.4 fusion.27
  531.4 0.0 copy-start
  531.4 2.3 copy-done
  533.7 29.5 %convolution_convert_fusion.4 = bf16[4480,1280]{1,0:T(8,128)(2,1)} fusion(bf16[2048,4480]{1,0:T(8,128)(2,1)} %get-tuple-element.43, bf16[2048,1280]{1,0:T(8,128)(2,1)S(1)} %fusion.27), kind=kOutput, calls=%fused_computation.16 | convolution fusion | flops 23493836800 | bytes 35061760 | tf_op jit(solution)/shard_map/dot_general | solution.py:12
  563.2 0.0 reduce-scatter.9.cloned.1.call-update
  563.2 0.0 reduce-scatter.7.cloned.1.call-start
  563.3 0.7 reduce-scatter.7.cloned.1.call-update
  563.9 0.0 reduce-scatter.5.cloned.1.call-start
  564.0 0.5 reduce-scatter.5.cloned.1.call-update
  564.5 57.7 %fusion.5 = (bf16[2048,4480]{1,0:T(8,128)(2,1)}, bf16[2048,4480]{1,0:T(8,128)(2,1)}) fusion(f32[2048,4480]{1,0:T(8,128)} %get-tuple-element.66, f32[2048,4480]{1,0:T(8,128)} %get-tuple-element.65, bf16[2048,1280]{1,0:T(8,128)(2,1)} %copy-done, bf16[4480,1280]{1,0:T(8,128)(2,1)} %get-tuple-element.64), kind=kOutput, calls=%fused_computation.9 | convolution fusion | flops 23625728000 | bytes 126812160 | tf_op jit(solution)/shard_map/dot_general | solution.py:12
  622.2 163.5 %sums.1 = (bf16[160,4480]{1,0:T(8,128)(2,1)}, bf16[160,4480]{1,0:T(8,128)(2,1)}) custom-call(bf16[2048,1280]{1,0:T(8,128)(2,1)} %get-tuple-element.42.a, bf16[2048,4480]{1,0:T(8,128)(2,1)} %get-tuple-element.67.by_gate, bf16[2048,4480]{1,0:T(8,128)(2,1)} %get-tuple-element.68.by_up), custom_call_target="tpu_custom_call" | custom-call | flops 46976204800 | bytes 60000000 | tf_op jit(solution)/shard_map/sums/pallas_call | solution.py:421
  785.7 0.0 reduce-scatter.11.cloned.1.call-done
  785.7 0.0 reduce-scatter.9.cloned.1.call-done
  785.7 0.0 copy-start.1
  785.8 16.8 %fusion.22 = (bf16[2,560,1280]{2,1,0:T(8,128)(2,1)}, f32[2,560,1280]{2,1,0:T(8,128)}, f32[2,560,1280]{2,1,0:T(8,128)}) fusion(bf16[2,560,1280]{2,1,0:T(8,128)(2,1)} %d.1, bf16[1,560,1280]{2,1,0:T(8,128)(2,1)} %bitcast.27, bf16[1,560,1280]{2,1,0:T(8,128)(2,1)} %bitcast.30, f32[2,560,1280]{2,1,0:T(8,128)} %param.21, f32[2,560,1280]{2,1,0:T(8,128)} %param.18), kind=kLoop, calls=%fused_computation.52 | loop fusion | flops 27238400 | bytes 31539200 | tf_op jit(solution)/shard_map/convert_element_type | solution.py:36
  802.6 0.0 reduce-scatter.7.cloned.1.call-done
  802.6 0.0 copy-done.1
  802.6 10.1 %fusion.18 = (bf16[2,160,4480]{2,1,0:T(8,128)(2,1)}, f32[2,160,4480]{2,1,0:T(8,128)}, f32[2,160,4480]{2,1,0:T(8,128)}) fusion(bf16[2,160,4480]{2,1,0:T(8,128)(2,1)S(1)} %copy-done.1, bf16[1,160,4480]{2,1,0:T(8,128)(2,1)} %bitcast.29, bf16[1,160,4480]{2,1,0:T(8,128)(2,1)} %bitcast.32, f32[2,160,4480]{2,1,0:T(8,128)} %param.20, f32[2,160,4480]{2,1,0:T(8,128)} %param.17), kind=kLoop, calls=%fused_computation.48 | loop fusion | flops 27238400 | bytes 31539200 | tf_op jit(solution)/shard_map/convert_element_type | solution.py:36
  812.7 45.4 %reduce-scatter.5.cloned.1.call-done = bf16[160,4480]{1,0:T(8,128)(2,1)} async-done(((bf16[1280,4480]{1,0:T(8,128)(2,1)}), bf16[160,4480]{1,0:T(8,128)(2,1)}) %reduce-scatter.5.cloned.1.call-update) | async-done | bytes 1433616 | tf_op jit(solution)/shard_map/reduce_scatter | solution.py:445
  858.1 10.3 %fusion.14 = (bf16[2,160,4480]{2,1,0:T(8,128)(2,1)}, f32[2,160,4480]{2,1,0:T(8,128)}, f32[2,160,4480]{2,1,0:T(8,128)}) fusion(bf16[2,160,4480]{2,1,0:T(8,128)(2,1)} %g.1, bf16[1,160,4480]{2,1,0:T(8,128)(2,1)} %bitcast.28, bf16[1,160,4480]{2,1,0:T(8,128)(2,1)} %bitcast.31, f32[2,160,4480]{2,1,0:T(8,128)} %param.19, f32[2,160,4480]{2,1,0:T(8,128)} %param.16), kind=kLoop, calls=%fused_computation.44 | loop fusion | flops 27238400 | bytes 31539200 | tf_op jit(solution)/shard_map/convert_element_type | solution.py:36
  (1 shorter events, 0.0 us)
Async XLA Ops:
  7.2 778.5 %reduce-scatter.11.cloned.1.call-start = ((), (), s32[]{:S(2)}) async-start(), calls=%async_computation.7 | async-start | bytes 12902400 | tf_op jit(solution)/shard_map/reduce_scatter | solution.py:445
  340.3 445.4 %reduce-scatter.9.cloned.1.call-start = ((), (), s32[]{:S(2)}) async-start(), calls=%async_computation.6 | async-start | bytes 12902400 | tf_op jit(solution)/shard_map/reduce_scatter | solution.py:445
  531.4 2.4 copy-start
  563.2 239.4 %reduce-scatter.7.cloned.1.call-start = ((), (), s32[]{:S(2)}) async-start(), calls=%async_computation.5 | async-start | bytes 12902400 | tf_op jit(solution)/shard_map/reduce_scatter | solution.py:445
  563.9 294.1 %reduce-scatter.5.cloned.1.call-start = ((), (), s32[]{:S(2)}) async-start(), calls=%async_computation.4 | async-start | bytes 12902400 | tf_op jit(solution)/shard_map/reduce_scatter | solution.py:445
  785.7 16.8 %copy-start.1 = (bf16[2,160,4480]{2,1,0:T(8,128)(2,1)S(1)}, bf16[2,160,4480]{2,1,0:T(8,128)(2,1)}, u32[]{:S(2)}) copy-start(bf16[2,160,4480]{2,1,0:T(8,128)(2,1)} %u.1) | copy-start | bytes 8601604
Sparse Core Ops, SparseCore 0:
  340.4 78.6 reduce-scatter.10
  563.3 80.3 reduce-scatter.8
  647.1 129.0 reduce-scatter.6
  779.5 78.4 reduce-scatter.4

commit v2 on v1

--- a/solution.py
+++ b/solution.py
@@ -74,7 +74,6 @@
         self.rows = shard.shape[0]
         first = -(-self.rows // 32) * 16
         self.halves = ((0, first), (first, self.rows - first))
-        self.sent = []
 
     def part(self, number, half):
         start, size = self.halves[half] if half is not None else (0, self.rows)
@@ -90,17 +89,11 @@
         pltpu.make_async_copy(self.shard, self.buffer, self.local.at[0]).start()
         for slot, half, axis in ((0, 0, SIDE_X), (2, 1, SIDE_Y), (1, 1, SIDE_X), (3, 0, SIDE_Y)):
             start, size = self.halves[half]
-            copy = self.remote(self.shard.at[pl.ds(start, size)], self.me, half, axis, slot)
-            copy.start()
-            self.sent.append(copy)
-        copy = self.remote(self.shard, self.me, None, CORE, 4)
-        copy.start()
-        self.sent.append(copy)
+            self.remote(self.shard.at[pl.ds(start, size)], self.me, half, axis, slot).start()
+        self.remote(self.shard, self.me, None, CORE, 4).start()
 
     def forward(self, number, half, axis, slot):
-        copy = self.remote(self.part(number, half), number, half, axis, slot)
-        copy.start()
-        self.sent.append(copy)
+        self.remote(self.part(number, half), number, half, axis, slot).start()
 
     def got(self, number, half, slot):
         self.remote(self.part(number, half), number, half, CORE, slot).wait_recv()
@@ -127,8 +120,8 @@
         pltpu.make_async_copy(self.buffer, self.part(me, None), self.local.at[1]).wait()
 
     def close(self):
-        for copy in self.sent:
-            copy.wait_send()
+        for slot, half in enumerate((0, 1, 1, 0, None, 1, 0, 0, 1, 1, 0, 0, 1)):
+            self.remote(self.part(self.me, half), self.me, half, CORE, slot).wait_send()
 
 
 def bring(source, target, sem):
@@ -161,20 +154,32 @@
         value = value.astype(F32)
         return (value * lax.rsqrt(jnp.mean(value**2, -1, keepdims=True) + 1e-6)).astype(BF16)
 
-    def gate_part(weight, gate, first, count):
+    def midway(number):
+        gathers[number].relay()
+        if number + 1 < len(gathers):
+            gathers[number + 1].begin()
+
+    def midway_at(number, tile):
+        @pl.when(pl.program_id(0) == tile)
+        def _():
+            midway(number)
+
+    def gate_stage(number, weight, gate):
         def body(w_tile, gate_tile):
+            midway_at(number, 3)
+
             @pl.loop(0, tokens // TALL)
             def _(i):
                 gate_tile[tall(i), :] = jnp.dot(states[tall(i), :], w_tile[...], preferred_element_type=F32)
 
-        pltpu.emit_pipeline(
-            body, grid=(count,),
-            in_specs=[pl.BlockSpec((depth, TILE), lambda j: (0, j + first))],
-            out_specs=[pl.BlockSpec((tokens, TILE), lambda j: (0, j + first))],
-        )(weight, gate)
-
-    def up_part(weight, gate, up, hidden, first, count):
+        spec = pl.BlockSpec((tokens, TILE), lambda j: (0, j))
+        pltpu.emit_pipeline(body, grid=(wide // TILE,), in_specs=[pl.BlockSpec((depth, TILE), lambda j: (0, j))], out_specs=[spec])(weight, gate)
+        gathers[number].finish()
+
+    def up_stage(number, weight, gate, up, hidden):
         def body(w_tile, gate_tile, up_tile, hidden_tile):
+            midway_at(number, 3)
+
             @pl.loop(0, tokens // TALL)
             def _(i):
                 value = jnp.dot(states[tall(i), :], w_tile[...], preferred_element_type=F32)
@@ -182,26 +187,25 @@
                 gate_value = gate_tile[tall(i), :]
                 hidden_tile[tall(i), :] = (gate_value * jax.nn.sigmoid(gate_value) * value).astype(BF16)
 
-        spec = pl.BlockSpec((tokens, TILE), lambda j: (0, j + first))
+        spec = pl.BlockSpec((tokens, TILE), lambda j: (0, j))
         pltpu.emit_pipeline(
-            body, grid=(count,),
-            in_specs=[pl.BlockSpec((depth, TILE), lambda j: (0, j + first)), spec],
-            out_specs=[spec, spec],
+            body, grid=(wide // TILE,), in_specs=[pl.BlockSpec((depth, TILE), lambda j: (0, j)), spec], out_specs=[spec, spec]
         )(weight, gate, up, hidden)
-
-    def down_part(first, count):
+        gathers[number].finish()
+
+    def down_stage(number):
         def body(hidden_tile, x_tile, h_tile, a_tile):
+            midway_at(number, 5)
             out = jnp.dot(hidden_tile[...], down[...], preferred_element_type=F32).astype(BF16)
             h = x_tile[...] + out
             h_tile[...] = h
             a_tile[...] = norm_of(h)
 
-        spec = pl.BlockSpec((ROWS, depth), lambda i: (i + first, 0))
+        spec = pl.BlockSpec((ROWS, depth), lambda i: (i, 0))
         pltpu.emit_pipeline(
-            body, grid=(count,),
-            in_specs=[pl.BlockSpec((ROWS, wide), lambda i: (i + first, 0)), spec],
-            out_specs=[spec, spec],
+            body, grid=(chunks,), in_specs=[pl.BlockSpec((ROWS, wide), lambda i: (i, 0)), spec], out_specs=[spec, spec]
         )(hidden0, x, h1, a1)
+        gathers[number].finish()
 
     meet(me, across)
     gathers[0].begin()
@@ -213,26 +217,15 @@
 
     bring(states, a0, sem)
 
-    def step(number, first_part, last_part):
-        if first_part is not None:
-            first_part()
-        gathers[number].relay()
-        if number + 1 < len(gathers):
-            gathers[number + 1].begin()
-        if last_part is not None:
-            last_part()
-        gathers[number].finish()
-
-    tiles = wide // TILE
-    most = (tiles + 1) // 2
-    step(0, None, None)
-    step(1, lambda: gate_part(full_g0, gate0, 0, most), lambda: gate_part(full_g0, gate0, most, tiles - most))
-    step(2, lambda: up_part(full_u0, gate0, up0, hidden0, 0, most), lambda: up_part(full_u0, gate0, up0, hidden0, most, tiles - most))
+    midway(0)
+    gathers[0].finish()
+    gate_stage(1, full_g0, gate0)
+    up_stage(2, full_u0, gate0, up0, hidden0)
     bring(full_d0, down, sem)
-    step(3, lambda: down_part(0, chunks // 2), lambda: down_part(chunks // 2, chunks // 2))
+    down_stage(3)
     bring(a1, states, sem)
-    step(4, lambda: gate_part(full_g1, gate1, 0, most), lambda: gate_part(full_g1, gate1, most, tiles - most))
-    step(5, lambda: up_part(full_u1, gate1, up1, hidden1, 0, most), lambda: up_part(full_u1, gate1, up1, hidden1, most, tiles - most))
+    gate_stage(4, full_g1, gate1)
+    up_stage(5, full_u1, gate1, up1, hidden1)
     for gather in gathers:
         gather.close()
 
@@ -260,27 +253,63 @@
             pltpu.VMEM(small, BF16), pltpu.VMEM(small, BF16), pltpu.VMEM(tall, BF16), pltpu.VMEM(tall, BF16),
             pltpu.SemaphoreType.DMA((6, 2)), pltpu.SemaphoreType.DMA((6, 13)), pltpu.SemaphoreType.DMA((6, 13)), pltpu.SemaphoreType.DMA,
         ],
-        compiler_params=pltpu.CompilerParams(collective_id=0, has_side_effects=True, vmem_limit_bytes=66_000_000),
+        compiler_params=pltpu.CompilerParams(collective_id=0, has_side_effects=True, vmem_limit_bytes=67_000_000),
         cost_estimate=pl.CostEstimate(flops=10 * tokens * depth * wide, bytes_accessed=300_000_000, transcendentals=0),
     )(x, w_gate, w_up, w_down)
 
 
 HELD, SLOTS = 6, 4
-
-
-def sums_kernel(a, by_gate, by_up, mine_g, mine_u, states, tiles, terms, out, core_out, core_in, far_out, far_in, near_out, near_in, local, core_s, core_r, far_s, far_r, near_s, near_r):
+SHORT = 512
+CUT = 640
+
+
+def sums_kernel(
+    a, by_out, down, gate, up, mine_g, mine_u, states, outer, downs, inner, tiles, terms, out,
+    core_out, core_in, far_out, far_in, near_out, near_in, local, core_s, core_r, far_s, far_r, near_s, near_r,
+):
     me, across = place()
-    _, depth = states.shape
+    tokens, depth = states.shape
     block = depth // 8
     half = block // 2
-    count = by_gate.shape[1] // TILE
-    sources, outs = (by_gate, by_up), (mine_g, mine_u)
+    count = -(-gate.shape[1] // CUT)
+    spare = count * CUT - gate.shape[1]
+    outs = (mine_g, mine_u)
+    chunks = tokens // SHORT
 
     def columns(j):
-        return pl.ds(pl.multiple_of(j * TILE, 128), TILE)
-
-    def load(p, j):
-        return pltpu.make_async_copy(sources[p].at[:, columns(j)], tiles.at[p], local.at[p])
+        return pl.ds(pl.multiple_of(j * CUT - j // (count - 1) * spare, 128), CUT)
+
+    def down_load(j):
+        slot = lax.rem(j, 2)
+        return pltpu.make_async_copy(down.at[columns(j)], downs.at[slot], local.at[3 + slot])
+
+    def inner_load(c, which):
+        slot = lax.rem(c, 2)
+        part = pl.ds(pl.multiple_of(lax.rem(c, chunks) * SHORT, SHORT), SHORT)
+        return pltpu.make_async_copy((gate, up)[which].at[part, columns(c // chunks)], inner.at[slot, which], local.at[5 + 2 * slot + which])
+
+    def inner_back(j):
+        down_load(j).wait()
+
+        @pl.when(j + 1 < count)
+        def _():
+            down_load(j + 1).start()
+
+        @pl.loop(0, chunks)
+        def _(r):
+            c = chunks * j + r
+            slot = lax.rem(c, 2)
+            for which in (0, 1):
+                inner_load(c, which).wait()
+
+            @pl.when(c + 1 < chunks * count)
+            def _():
+                for which in (0, 1):
+                    inner_load(c + 1, which).start()
+
+            part = pl.ds(pl.multiple_of(r * SHORT, SHORT), SHORT)
+            by = dot(outer[part, :], downs[lax.rem(j, 2)], ((1,), (1,))).astype(BF16)
+            tiles[0, part, :], tiles[1, part, :] = gates_back(by, inner[slot, 0], inner[slot, 1])
 
     def rows(number, start=0, size=block):
         return pl.ds(pl.multiple_of(number * block + start, 16), size)
@@ -305,8 +334,7 @@
 
     blocks = (0, SIDE_X, SIDE_Y, SIDE_X | SIDE_Y)
 
-    def multiply(t, p, j):
-        load(p, j).wait()
+    def multiply(t, p):
         held = lax.rem(t, HELD)
 
         @pl.loop(0, depth // TILE)
@@ -315,10 +343,6 @@
             terms[held, part, :] = lax.dot_general(
                 states[:, part], tiles[p], (((0,), (0,)), ((), ())), preferred_element_type=F32
             )
-
-        @pl.when(j + 1 < count)
-        def _():
-            load(p, j + 1).start()
 
     def to_core(t):
         slot, held = lax.rem(t, SLOTS), lax.rem(t, HELD)
@@ -375,8 +399,10 @@
         out[p, :, columns(j)] = total.astype(BF16)
 
     meet(me, across)
-    load(0, 0).start()
-    load(1, 0).start()
+    down_load(0).start()
+    for which in (0, 1):
+        inner_load(0, which).start()
+    bring(by_out, outer, local.at[1])
     bring(a, states, local.at[2])
 
     @pl.loop(0, count + 3)
@@ -386,7 +412,9 @@
 
             @pl.when(j < count)
             def _():
-                multiply(t, p, j)
+                if p == 0:
+                    inner_back(j)
+                multiply(t, p)
 
             def stage(lag, run):
                 q = (p - lag) % 2
@@ -413,31 +441,32 @@
         bring(out.at[p], outs[p], local.at[2])
 
 
-def sums(a, by_gate, by_up):
+def sums(a, by_out, down, gate, up):
     tokens, depth = a.shape
-    wide = by_gate.shape[1]
+    wide = gate.shape[1]
     block = depth // 8
     anywhere = pl.BlockSpec(memory_space=pl.ANY)
     return pl.pallas_call(
         sums_kernel,
         name="sums",
         out_shape=[jax.ShapeDtypeStruct((block, wide), BF16)] * 2,
-        in_specs=[anywhere] * 3,
+        in_specs=[anywhere] * 5,
         out_specs=[anywhere] * 2,
         scratch_shapes=[
-            pltpu.VMEM((tokens, depth), BF16), pltpu.VMEM((2, tokens, TILE), BF16), pltpu.VMEM((HELD, depth, TILE), F32),
+            pltpu.VMEM((tokens, depth), BF16), pltpu.VMEM((tokens, depth), BF16), pltpu.VMEM((2, CUT, depth), BF16),
+            pltpu.VMEM((2, 2, SHORT, CUT), F32), pltpu.VMEM((2, tokens, CUT), BF16), pltpu.VMEM((HELD, depth, CUT), F32),
             pltpu.VMEM((2, block, wide), BF16),
-            pltpu.VMEM((SLOTS, 4, block, TILE), BF16), pltpu.VMEM((SLOTS, 4, block, TILE), BF16),
-            pltpu.VMEM((SLOTS, 2, block // 2, TILE), BF16), pltpu.VMEM((SLOTS, 2, block // 2, TILE), BF16),
-            pltpu.VMEM((SLOTS, 2, block, TILE), BF16), pltpu.VMEM((SLOTS, 2, block, TILE), BF16),
-            pltpu.SemaphoreType.DMA((3,)),
+            pltpu.VMEM((SLOTS, 4, block, CUT), BF16), pltpu.VMEM((SLOTS, 4, block, CUT), BF16),
+            pltpu.VMEM((SLOTS, 2, block // 2, CUT), BF16), pltpu.VMEM((SLOTS, 2, block // 2, CUT), BF16),
+            pltpu.VMEM((SLOTS, 2, block, CUT), BF16), pltpu.VMEM((SLOTS, 2, block, CUT), BF16),
+            pltpu.SemaphoreType.DMA((9,)),
             pltpu.SemaphoreType.DMA((SLOTS,)), pltpu.SemaphoreType.DMA((SLOTS,)),
             pltpu.SemaphoreType.DMA((SLOTS, 2)), pltpu.SemaphoreType.DMA((SLOTS, 2)),
             pltpu.SemaphoreType.DMA((SLOTS, 2)), pltpu.SemaphoreType.DMA((SLOTS, 2)),
         ],
-        compiler_params=pltpu.CompilerParams(collective_id=1, has_side_effects=True, vmem_limit_bytes=66_000_000),
-        cost_estimate=pl.CostEstimate(flops=4 * tokens * depth * wide, bytes_accessed=60_000_000, transcendentals=0),
-    )(a, by_gate, by_up)
+        compiler_params=pltpu.CompilerParams(collective_id=1, has_side_effects=True, vmem_limit_bytes=67_000_000),
+        cost_estimate=pl.CostEstimate(flops=6 * tokens * depth * wide, bytes_accessed=100_000_000, transcendentals=0),
+    )(a, by_out, down, gate, up)
 
 
 def solution(mesh):
@@ -468,9 +497,7 @@
         by_d0 = dot(hidden0, by_h1, rows).astype(BF16)
         by_d0, by_h1, gate0, up0 = after(by_d0, by_h1, gate0, up0)
         mine_d0 = scatter(by_d0)
-        by_hidden0 = dot(by_h1, d0, ((1,), (1,))).astype(BF16)
-        by_gate0, by_up0 = after(*gates_back(by_hidden0, gate0, up0))
-        mine_g0, mine_u0 = sums(a0, by_gate0, by_up0)
+        mine_g0, mine_u0 = sums(a0, by_h1, d0, gate0, up0)
 
         gradients = [jnp.stack(pair).astype(F32) for pair in ((mine_g0, mine_g1), (mine_u0, mine_u1), (mine_d0, mine_d1))]
         new = [adamw(w.astype(F32), m, v, g) for w, m, v, g in zip(weights, m, v, gradients, strict=True)]

time: 884 us -> 882 us (level)
  matrix products: 301 us -> 243 us
  waiting for transfers between devices: 46.7 us -> 80.5 us
  Pallas kernels: 466 us -> 493 us
    dot_general x8 -> x7, matrix products: 301 us -> 243 us  [dot(): return lax.dot_general(a, w, (dims, ((), ())), preferred_element_type=F32)]
    pallas_call x1, Pallas kernels: 163 us -> 198 us  [sums(): pl.pallas_call(sums_kernel, name='sums', out_shape=[jax.ShapeDtypeStruct(...]
    reduce_scatter x4, waiting for transfers between devices: 45.4 us -> 79.3 us  [scatter(): return lax.psum_scatter(g, 'dp', scatter_dimension=0, tiled=True)]
  transfers between devices with their start and end apart: 4 -> 4, of which waited for: 1 -> 2; matrix products, arithmetic and copies ran while one was open for 35% -> 28% of each run, Pallas kernels for 19% -> 23%
where the time goes in v2:
time: 882 us; the launch traced here: 874 us
  Pallas kernels  493 us (56%)
  matrix products  243 us (28%)
  waiting for transfers between devices  80.5 us (9%)
  other arithmetic  41.2 us (5%)
  between operations  14.3 us (2%)
    pallas_call x1, Pallas kernels, forward(): pl.pallas_call(forward_kernel, name='forward', out_shape=shapes, in_specs...  295 us
    dot_general x7, matrix products, dot(): return lax.dot_general(a, w, (dims, ((), ())), preferred_element_type=F32)  243 us
    pallas_call x1, Pallas kernels, sums(): pl.pallas_call(sums_kernel, name='sums', out_shape=[jax.ShapeDtypeStruct(...  198 us
    reduce_scatter x4, waiting for transfers between devices, scatter(): return lax.psum_scatter(g, 'dp', scatter_dimension=0, tiled=True)  79.3 us
    convert_element_type x3, other arithmetic, adamw(): return ((w - 0.02 * step).astype(BF16), m, v)  33.8 us
  transfers between devices with their start and end apart: 4, of which 2 were waited for; matrix products, arithmetic and copies ran while one was open for 28% of the time, Pallas kernels for 23%

profile of v2, /device:TPU:0, one launch (start us, length us, event | category | flops | bytes accessed | tf_op | source)
XLA Modules:
  0.0 874.4 jit_solution(8733565551413961580)
XLA Ops:
  7.2 0.0 reduce-scatter.11.cloned.1.call-start
  7.2 295.1 %forward.1 = (bf16[1280,4480]{1,0:T(8,128)(2,1)}, bf16[1280,4480]{1,0:T(8,128)(2,1)}, bf16[4480,1280]{1,0:T(8,128)(2,1)}, bf16[1280,4480]{1,0:T(8,128)(2,1)}, bf...) custom-call(bf16[2048,1280]{1,0:T(8,128)(2,1)} %bitcast.31, ...), custom_call_target="tpu_custom_call" | custom-call | flops 117440512000 | bytes 300000000 | tf_op jit(solution)/shard_map/forward/pallas_call | solution.py:245
  302.3 30.2 %convolution_convert_fusion.4 = bf16[4480,1280]{1,0:T(8,128)(2,1)} fusion(bf16[2048,4480]{1,0:T(8,128)(2,1)} %get-tuple-element.43, bf16[1,2048,1280]{2,1,0:T(8,128)(2,1)} %param.12), kind=kOutput, calls=%fused_computation.10 | convolution fusion | flops 23493836800 | bytes 35061760 | tf_op jit(solution)/shard_map/dot_general | solution.py:12
  332.6 0.0 reduce-scatter.11.cloned.1.call-update
  332.6 0.0 reduce-scatter.9.cloned.1.call-start
  332.6 54.2 %fusion.2 = (bf16[2048,4480]{1,0:T(8,128)(2,1)}, bf16[2048,4480]{1,0:T(8,128)(2,1)}) fusion(f32[2048,4480]{1,0:T(8,128)} %get-tuple-element.49, f32[2048,4480]{1,0:T(8,128)} %get-tuple-element.48, bf16[2048,1280]{1,0:T(8,128)(2,1)} %bitcast.24, bf16[4480,1280]{1,0:T(8,128)(2,1)} %get-tuple-element.47), kind=kOutput, calls=%fused_computation.4 | convolution fusion | flops 23625728000 | bytes 126812160 | tf_op jit(solution)/shard_map/dot_general | solution.py:12
  386.8 32.0 %convolution_convert_fusion.1 = bf16[1280,4480]{1,0:T(8,128)(2,1)} fusion(bf16[2048,1280]{1,0:T(8,128)(2,1)} %get-tuple-element.42, bf16[2048,4480]{1,0:T(8,128)(2,1)} %get-tuple-element.54), kind=kOutput, calls=%fused_computation.7 | convolution fusion | flops 23493836800 | bytes 35061760 | tf_op jit(solution)/shard_map/dot_general | solution.py:12
  418.8 31.6 %convolution_convert_fusion = bf16[1280,4480]{1,0:T(8,128)(2,1)} fusion(bf16[2048,1280]{1,0:T(8,128)(2,1)} %get-tuple-element.42, bf16[2048,4480]{1,0:T(8,128)(2,1)} %get-tuple-element.56), kind=kOutput, calls=%fused_computation.6 | convolution fusion | flops 23493836800 | bytes 35061760 | tf_op jit(solution)/shard_map/dot_general | solution.py:12
  450.4 31.8 %convolution_convert_fusion.5 = bf16[2048,1280]{1,0:T(8,128)(2,1)} fusion(bf16[2048,4480]{1,0:T(8,128)(2,1)} %get-tuple-element.56, bf16[1280,4480]{1,0:T(8,128)(2,1)} %get-tuple-element.57), kind=kOutput, calls=%fused_computation.23 | convolution fusion | flops 23490723840 | bytes 35061760 | tf_op jit(solution)/shard_map/dot_general | solution.py:12
  482.2 33.6 %fusion.5 = (f32[2048]{0:T(1024)S(1)}, f32[2048]{0:T(1024)S(1)}, bf16[2048,1280]{1,0:T(8,128)(2,1)}) fusion(bf16[2048,1280]{1,0:T(8,128)(2,1)} %get-tuple-element.58, bf16[2048,1280]{1,0:T(8,128)(2,1)} %convolution_convert_fusion.5, bf16[2048,4480]{1,0:T(8,128)(2,1)} %get-tuple-element.54, bf16[1280,4480]{1,0:T(8,128)(2,1)} %get-tuple-element.55), kind=kOutput, calls=%fused_computation.17 | convolution fusion | flops 23509069824 | bytes 45563904 | tf_op jit(solution)/shard_map/dot_general | solution.py:12
  515.8 7.4 fusion.24.by_out
  523.2 0.0 copy-start
  523.2 2.3 copy-done
  525.6 29.4 %convolution_convert_fusion.3 = bf16[4480,1280]{1,0:T(8,128)(2,1)} fusion(bf16[2048,4480]{1,0:T(8,128)(2,1)} %get-tuple-element.41, bf16[2048,1280]{1,0:T(8,128)(2,1)S(1)} %fusion.24.by_out), kind=kOutput, calls=%fused_computation.9 | convolution fusion | flops 23493836800 | bytes 35061760 | tf_op jit(solution)/shard_map/dot_general | solution.py:12
  555.0 0.0 reduce-scatter.9.cloned.1.call-update
  555.0 0.0 reduce-scatter.7.cloned.1.call-start
  555.1 0.7 reduce-scatter.7.cloned.1.call-update
  555.8 0.0 reduce-scatter.5.cloned.1.call-start
  555.8 0.5 reduce-scatter.5.cloned.1.call-update
  556.3 198.0 %sums.1 = (bf16[160,4480]{1,0:T(8,128)(2,1)}, bf16[160,4480]{1,0:T(8,128)(2,1)}) custom-call(bf16[2048,1280]{1,0:T(8,128)(2,1)} %get-tuple-element.40.a, bf16[2048,1280]{1,0:T(8,128)(2,1)} %copy-done, bf16[4480,1280]{1,0:T(8,128)(2,1)} %get-tuple-element.62.down, f32[2048,4480]{1,0:T(8,128)} %get-tuple-element.63.gate, f32[2048,4480]{1,0:T(8,128)} %get-tuple-element.64.up), custom_call_target="tpu_custom_call" | custom-call | flops 70464307200 | bytes 100000000 | tf_op jit(solution)/shard_map/sums/pallas_call | solution.py:449
  754.4 0.0 reduce-scatter.11.cloned.1.call-done
  754.4 0.0 reduce-scatter.9.cloned.1.call-done
  754.4 0.0 copy-start.1
  754.5 11.5 %fusion.19 = (bf16[2,560,1280]{2,1,0:T(8,128)(2,1)}, f32[2,560,1280]{2,1,0:T(8,128)}, f32[2,560,1280]{2,1,0:T(8,128)}) fusion(bf16[2,560,1280]{2,1,0:T(8,128)(2,1)} %d.1, bf16[1,560,1280]{2,1,0:T(8,128)(2,1)} %bitcast.25, bf16[1,560,1280]{2,1,0:T(8,128)(2,1)} %bitcast.28, f32[2,560,1280]{2,1,0:T(8,128)} %param.21, f32[2,560,1280]{2,1,0:T(8,128)} %param.18), kind=kLoop, calls=%fused_computation.45 | loop fusion | flops 27238400 | bytes 31539200 | tf_op jit(solution)/shard_map/convert_element_type | solution.py:36
  766.0 9.3 %reduce-scatter.7.cloned.1.call-done = bf16[160,4480]{1,0:T(8,128)(2,1)} async-done(((bf16[1280,4480]{1,0:T(8,128)(2,1)}), bf16[160,4480]{1,0:T(8,128)(2,1)}) %reduce-scatter.7.cloned.1.call-update) | async-done | bytes 1433616 | tf_op jit(solution)/shard_map/reduce_scatter | solution.py:474
  775.3 0.0 copy-done.1
  775.3 12.0 %fusion.15 = (bf16[2,160,4480]{2,1,0:T(8,128)(2,1)}, f32[2,160,4480]{2,1,0:T(8,128)}, f32[2,160,4480]{2,1,0:T(8,128)}) fusion(bf16[2,160,4480]{2,1,0:T(8,128)(2,1)S(1)} %copy-done.1, bf16[1,160,4480]{2,1,0:T(8,128)(2,1)} %bitcast.27, bf16[1,160,4480]{2,1,0:T(8,128)(2,1)} %bitcast.30, f32[2,160,4480]{2,1,0:T(8,128)} %param.20, f32[2,160,4480]{2,1,0:T(8,128)} %param.17), kind=kLoop, calls=%fused_computation.41 | loop fusion | flops 27238400 | bytes 31539200 | tf_op jit(solution)/shard_map/convert_element_type | solution.py:36
  787.2 69.9 %reduce-scatter.5.cloned.1.call-done = bf16[160,4480]{1,0:T(8,128)(2,1)} async-done(((bf16[1280,4480]{1,0:T(8,128)(2,1)}), bf16[160,4480]{1,0:T(8,128)(2,1)}) %reduce-scatter.5.cloned.1.call-update) | async-done | bytes 1433616 | tf_op jit(solution)/shard_map/reduce_scatter | solution.py:474
  857.1 10.3 %fusion.11 = (bf16[2,160,4480]{2,1,0:T(8,128)(2,1)}, f32[2,160,4480]{2,1,0:T(8,128)}, f32[2,160,4480]{2,1,0:T(8,128)}) fusion(bf16[2,160,4480]{2,1,0:T(8,128)(2,1)} %g.1, bf16[1,160,4480]{2,1,0:T(8,128)(2,1)} %bitcast.26, bf16[1,160,4480]{2,1,0:T(8,128)(2,1)} %bitcast.29, f32[2,160,4480]{2,1,0:T(8,128)} %param.19, f32[2,160,4480]{2,1,0:T(8,128)} %param.16), kind=kLoop, calls=%fused_computation.37 | loop fusion | flops 27238400 | bytes 31539200 | tf_op jit(solution)/shard_map/convert_element_type | solution.py:36
  (1 shorter events, 0.0 us)
Async XLA Ops:
  7.2 747.2 %reduce-scatter.11.cloned.1.call-start = ((), (), s32[]{:S(2)}) async-start(), calls=%async_computation.7 | async-start | bytes 12902400 | tf_op jit(solution)/shard_map/reduce_scatter | solution.py:474
  332.6 421.8 %reduce-scatter.9.cloned.1.call-start = ((), (), s32[]{:S(2)}) async-start(), calls=%async_computation.6 | async-start | bytes 12902400 | tf_op jit(solution)/shard_map/reduce_scatter | solution.py:474
  523.2 2.4 copy-start
  555.0 220.3 %reduce-scatter.7.cloned.1.call-start = ((), (), s32[]{:S(2)}) async-start(), calls=%async_computation.5 | async-start | bytes 12902400 | tf_op jit(solution)/shard_map/reduce_scatter | solution.py:474
  555.8 301.4 %reduce-scatter.5.cloned.1.call-start = ((), (), s32[]{:S(2)}) async-start(), calls=%async_computation.4 | async-start | bytes 12902400 | tf_op jit(solution)/shard_map/reduce_scatter | solution.py:474
  754.4 20.8 %copy-start.1 = (bf16[2,160,4480]{2,1,0:T(8,128)(2,1)S(1)}, bf16[2,160,4480]{2,1,0:T(8,128)(2,1)}, u32[]{:S(2)}) copy-start(bf16[2,160,4480]{2,1,0:T(8,128)(2,1)} %u.1) | copy-start | bytes 8601604
Sparse Core Ops, SparseCore 0:
  332.7 78.5 reduce-scatter.10
  555.2 109.5 reduce-scatter.8
  668.2 107.0 reduce-scatter.6
  778.6 78.5 reduce-scatter.4
